TPU v7x, 32 devices: a whole 2x2x4 slice. The times are simulated.
32 devices in a mesh: gx: 4 (over x, core), gy: 8 (over z, y).
Axes of the slice: x: 2, y: 2, z: 4, core: 2. Of those that a mesh axis runs over, the one named last changes fastest.
Arguments:
- east_velocity: float32 [48, 32, 2048], P(None, 'gx', 'gy'), may hold values from -3 to 3
- north_velocity: float32 [48, 32, 2048], P(None, 'gx', 'gy'), may hold values from -3 to 3
- salinity: float32 [48, 32, 2048], P(None, 'gx', 'gy'), may hold values from -6 to 6
- surface: float32 [32, 2048], P('gx', 'gy'), may hold values from -6 to 6
- column_depth: float32 [32, 2048], P('gx', 'gy'), may hold values from 0.5 to 4
- wet_column: int32 [32, 2048], P('gx', 'gy'), may hold values 0 or 1
- active_levels: int32 [32, 2048], P('gx', 'gy'), may hold values from 1 to 48
Outputs:
- east_flow: float32 [48, 32, 2048], P(None, 'gx', 'gy')
- north_flow: float32 [48, 32, 2048], P(None, 'gx', 'gy')
- salt_next: float32 [48, 32, 2048], P(None, 'gx', 'gy')
- surface_next: float32 [32, 2048], P('gx', 'gy')
All inputs are finite; a program needn't handle non-finite values. No bound on the sum of `wet_column` on one device may be relied on, other than what follows from the above.
Results may differ from a plain program's by a relative error of at most 0.000024.
Values sent between devices are 32-bit elements; how exact they have to be, the bound alone decides.
A program may use at most 64 MiB of HBM per device.

v0:
```python
import functools

import jax
import jax.numpy as jnp
from jax import lax
from jax.experimental import pallas as pl
from jax.experimental.pallas import tpu as pltpu
from jax.sharding import PartitionSpec as P

ITERS = 16

TIME_STEP = 0.2
CORIOLIS = 0.3
PRESS_COEF = 0.05
VISCOSITY = 0.1
DIFFUSIVITY = 0.1
SIGMA_SHIFT = 0.25
CHEB_CENTER = 3.625
CHEB_HALF = 3.375
DIVERGENCE_COEF = 8.0

ROWS = 8
LANES = 128
CHUNK = 8
RIM = LANES // 4
MESH = pl.DeviceIdType.MESH


def cheb_table(count):
    first = CHEB_CENTER / CHEB_HALF
    ratio = 1.0 / first
    keeps = []
    gains = []
    for index in range(count):
        ratio_next = 1.0 / (2.0 * first - ratio)
        keeps.append(ratio_next * ratio)
        gains.append(2.0 * ratio_next / CHEB_HALF)
        ratio = ratio_next
    return (keeps, gains)


def dry_factor(count):
    keeps, gains = cheb_table(count)
    x, r = 1.0, -1.0
    d = r / CHEB_CENTER
    for index in range(count):
        x = x + d
        r = r - d
        d = keeps[index] * d + gains[index] * r
    return x


def kernel(
    nx, ny, reach, slots,
    east_hbm, north_hbm, salt_hbm, surface_hbm, depth_hbm, wet_hbm, active_hbm,
    state_out, slope_out, surface_out,
    held, moved, shifts, ints, floats, zeros, halo, send_x, send_y, far_c, far_e, gath, xs,
    load_sem, small_sem, halo_sem, side_sem, far_send, far_recv,
):
    gx = lax.axis_index("gx")
    gy = lax.axis_index("gy")
    width = held.shape[4]
    tiles = width // LANES
    chunks = held.shape[0] // 3
    levels = chunks * CHUNK
    groups = 3 * CHUNK // 4
    n = groups * tiles
    relative = slots < nx
    row = lax.broadcasted_iota(jnp.int32, (ROWS, LANES), 0)
    lane = lax.broadcasted_iota(jnp.int32, (ROWS, LANES), 1)
    pair = row // 2
    zero = jnp.zeros((ROWS, LANES), jnp.float32)

    def lanes(t):
        return slice(t * LANES, (t + 1) * LANES)

    def inside(x, y):
        return jnp.logical_and(
            jnp.logical_and(x >= 0, x < nx), jnp.logical_and(y >= 0, y < ny)
        )

    def whole(ref, sem):
        return pltpu.make_async_copy(ref, ref, sem)

    pltpu.make_async_copy(active_hbm, ints.at[0], small_sem.at[0]).start()
    pltpu.make_async_copy(wet_hbm, ints.at[1], small_sem.at[0]).start()
    for c in range(chunks):
        part = pl.ds(c * CHUNK, CHUNK)
        for f, source in enumerate((east_hbm, north_hbm, salt_hbm)):
            pltpu.make_async_copy(source.at[part], held.at[c, f], load_sem.at[c]).start()
    pltpu.make_async_copy(surface_hbm, floats.at[0], small_sem.at[1]).start()
    pltpu.make_async_copy(depth_hbm, floats.at[1], small_sem.at[1]).start()

    own = reach if relative else gx
    partners = [
        (o, side)
        for o in range(-reach, reach + 1)
        for side in (-1, 0, 1)
        if (o, side) != (0, 0)
    ]

    def far(action):
        for o, side in partners:
            @pl.when(inside(gx + o, gy + side))
            def _(o=o, side=side):
                action(o, side)

    barrier = pltpu.get_barrier_semaphore()
    count = jnp.int32(0)
    for o, side in partners:
        there = inside(gx + o, gy + side)

        @pl.when(there)
        def _(o=o, side=side):
            pl.semaphore_signal(
                barrier, inc=1, device_id=(gx + o, gy + side), device_id_type=MESH
            )

        count = count + there.astype(jnp.int32)

    for i in range(n):
        zeros[i] = zero

    source = lax.broadcasted_iota(jnp.int32, (width, width), 0)
    target = lax.broadcasted_iota(jnp.int32, (width, width), 1)
    step = source - target
    one = jnp.abs(step) == 1
    sign = jnp.where(step > 0, 1.0, -1.0)
    slope = jnp.where(one, 8.0 * sign, jnp.where(jnp.abs(step) == 2, -sign, 0.0))
    shifts[:, :width] = slope.astype(jnp.bfloat16)
    shifts[:, width:] = jnp.where(one, 1.0, 0.0).astype(jnp.bfloat16)

    def move(index):
        value = held[index].reshape(3 * CHUNK * ROWS, width)
        high = value.astype(jnp.bfloat16)
        rest = value - high.astype(jnp.float32)
        middle = rest.astype(jnp.bfloat16)
        low = (rest - middle.astype(jnp.float32)).astype(jnp.bfloat16)
        total = jnp.dot(low, shifts[...], preferred_element_type=jnp.float32)
        total = total + jnp.dot(middle, shifts[...], preferred_element_type=jnp.float32)
        total = total + jnp.dot(high, shifts[...], preferred_element_type=jnp.float32)
        moved[index] = total.reshape(3, CHUNK, ROWS, 2 * width)

    def pack(stage, c):
        rim = zero
        for f in range(3):
            for half in range(CHUNK // 4):
                group = f * (CHUNK // 4) + half
                ups = [None] * tiles
                downs = [None] * tiles
                for m in range(4):
                    kk = half * 4 + m
                    position = group * 4 + m
                    parts = [
                        held[stage * chunks + c, f, kk, :, lanes(t)] for t in range(tiles)
                    ]
                    for t in range(tiles):
                        turned = parts[t] if m == 3 else pltpu.roll(parts[t], 2 * m + 2, 0)
                        if m == 0:
                            ups[t] = turned
                            downs[t] = turned
                        else:
                            ups[t] = jnp.where(pair == m, turned, ups[t])
                            downs[t] = jnp.where(pair == (m + 1) % 4, turned, downs[t])
                    ends = jnp.where(lane < LANES // 2, parts[0], parts[-1])
                    rim = jnp.where(
                        lane // 4 == position,
                        pltpu.roll(ends, (4 * position + 2) % LANES, 1),
                        rim,
                    )
                for t in range(tiles):
                    send_x[0, stage, c, group * tiles + t] = downs[t]
                    send_x[1, stage, c, group * tiles + t] = ups[t]
        send_y[stage, c, 0] = rim

    def x_copy(stage, c, side):
        return pltpu.make_async_remote_copy(
            src_ref=send_x.at[side, stage, c],
            dst_ref=halo.at[stage, c, pl.ds((1 - side) * n, n)],
            send_sem=side_sem.at[side],
            recv_sem=halo_sem.at[stage, c],
            device_id=(gx + 2 * side - 1, gy),
            device_id_type=MESH,
        )

    def y_copy(stage, c, side):
        return pltpu.make_async_remote_copy(
            src_ref=send_y.at[stage, c],
            dst_ref=halo.at[stage, c, pl.ds(2 * n + 1 - side, 1)],
            send_sem=side_sem.at[2 + side],
            recv_sem=halo_sem.at[stage, c],
            device_id=(gx, gy + 2 * side - 1),
            device_id_type=MESH,
        )

    near = [
        (x_copy, 0, gx > 0), (x_copy, 1, gx < nx - 1),
        (y_copy, 0, gy > 0), (y_copy, 1, gy < ny - 1),
    ]

    def launch(stage, c):
        for copy, side, there in near:
            @pl.when(there)
            def _(copy=copy, side=side):
                copy(stage, c, side).start()

    def far_start(kind):
        def action(o, side):
            slot = reach - o if relative else gx
            if side == 0:
                source, target = far_c.at[kind], gath.at[kind, slot, pl.ds(0, 2 * tiles)]
            else:
                at = 2 * tiles + (1 - side) // 2
                source, target = far_e.at[kind], gath.at[kind, slot, pl.ds(at, 1)]
            pltpu.make_async_remote_copy(
                src_ref=source, dst_ref=target,
                send_sem=far_send.at[side + 1, o + reach if relative else gx + o],
                recv_sem=far_recv.at[kind],
                device_id=(gx + o, gy + side), device_id_type=MESH,
            ).start()

        far(action)
        pltpu.make_async_copy(
            far_c.at[kind], gath.at[kind, own, pl.ds(0, 2 * tiles)], far_recv.at[kind]
        ).start()

    def far_drain(o, side):
        sem = far_send.at[side + 1, o + reach if relative else gx + o]
        whole(far_c if side == 0 else far_e, sem).wait()

    def fill_far(data):
        low, high = data
        first = jnp.where(lane < RIM, low[0], pltpu.roll(high[0], RIM, 1))
        second = jnp.where(
            lane < LANES - RIM, pltpu.roll(high[-1], LANES - RIM, 1), low[-1]
        )
        return jnp.where(lane < 2 * RIM, first, second)

    def put_far(kind, data):
        for f in range(2):
            for t in range(tiles):
                far_c[kind, f * tiles + t] = data[f][t]
        far_e[kind, 0] = fill_far(data)

    whole(ints, small_sem.at[0]).wait()
    active = [ints[0, :, lanes(t)] * ints[1, :, lanes(t)] for t in range(tiles)]

    def first(c):
        whole(held.at[c], load_sem.at[c]).wait()
        for kk in range(CHUNK):
            for t in range(tiles):
                live = active[t] > c * CHUNK + kk
                for f in range(3):
                    held[c, f, kk, :, lanes(t)] = jnp.where(
                        live, held[c, f, kk, :, lanes(t)], 0.0
                    )
        pack(0, c)

    first(0)
    pl.semaphore_wait(barrier, count)
    launch(0, 0)

    @pl.loop(1, chunks)
    def _(c):
        first(c)
        launch(0, c)
        move(c - 1)

    for side, missing in ((0, gx == 0), (1, gx == nx - 1)):
        @pl.when(missing)
        def _(side=side):
            for stage in range(3):
                @pl.loop(0, chunks)
                def _(c, stage=stage):
                    pltpu.make_async_copy(
                        zeros, halo.at[stage, c, pl.ds(side * n, n)], halo_sem.at[stage, c]
                    ).start()

    for side, missing in ((0, gy == 0), (1, gy == ny - 1)):
        @pl.when(missing)
        def _(side=side):
            for stage in range(3):
                @pl.loop(0, chunks)
                def _(c, stage=stage):
                    pltpu.make_async_copy(
                        zeros.at[pl.ds(0, 1)],
                        halo.at[stage, c, pl.ds(2 * n + side, 1)],
                        halo_sem.at[stage, c],
                    ).start()
            for j in range(slots):
                @pl.when(inside(gx + j - reach, gy) if relative else gy >= 0)
                def _(j=j):
                    for kind in range(2):
                        pltpu.make_async_copy(
                            zeros.at[pl.ds(0, 1)],
                            gath.at[kind, j, pl.ds(2 * tiles + side, 1)],
                            far_recv.at[kind],
                        ).start()

    if relative:
        for j in range(slots):
            @pl.when(jnp.logical_not(inside(gx + j - reach, gy)))
            def _(j=j):
                for kind in range(2):
                    pltpu.make_async_copy(
                        zeros.at[pl.ds(0, 2 * tiles + 2)], gath.at[kind, j], far_recv.at[kind]
                    ).start()

    whole(floats, small_sem.at[1]).wait()
    put_far(0, (
        [floats[0, :, lanes(t)] for t in range(tiles)],
        [ints[1, :, lanes(t)].astype(jnp.float32) for t in range(tiles)],
    ))

    quarter = lane % 4

    def run_stage(stage, weight0, weight1):
        gain = weight1 * TIME_STEP
        keep_flow = weight1 - 4.0 * gain * VISCOSITY
        keep_salt = weight1 - 4.0 * gain * DIFFUSIVITY
        drift = -gain / 12.0
        push = drift * PRESS_COEF

        def body(c, carry, behind=stage < 2):
            press_e, press_n = list(carry[0]), list(carry[1])
            sums = [list(x) for x in carry[2:]]
            index = stage * chunks + c
            whole(halo.at[stage, c], halo_sem.at[stage, c]).wait()
            if behind:
                move(index + chunks - 1)
            rims = jnp.where(quarter < 2, halo[stage, c, 2 * n], halo[stage, c, 2 * n + 1])
            r1, r2 = pltpu.roll(rims, LANES - 1, 1), pltpu.roll(rims, LANES - 2, 1)
            l1, l2 = pltpu.roll(rims, 1, 1), pltpu.roll(rims, 2, 1)
            rim_slope = jnp.where(
                quarter < 2,
                jnp.where(quarter == 0, -r2, 8.0 * r1 - r2),
                jnp.where(quarter == 2, l2 - 8.0 * l1, l2),
            )
            rim_sum = jnp.where(quarter == 1, r1, jnp.where(quarter == 2, l1, 0.0))
            for kk in range(CHUNK):
                fields = []
                for f in range(3):
                    position = f * CHUNK + kk
                    group, m = position // 4, position % 4
                    back = (-(4 * position + 2)) % LANES
                    extra_slope = pltpu.roll(rim_slope, back, 1)
                    extra_sum = pltpu.roll(rim_sum, back, 1)
                    per_tile = []
                    for t in range(tiles):
                        q = held[index, f, kk, :, lanes(t)]
                        ends = jnp.where(
                            pair == m,
                            halo[stage, c, group * tiles + t],
                            halo[stage, c, n + group * tiles + t],
                        )
                        if m != 3:
                            ends = pltpu.roll(ends, (-(2 * m + 2)) % ROWS, 0)
                        e1 = pltpu.roll(jnp.where(row < 1, ends, q), ROWS - 1, 0)
                        e2 = pltpu.roll(jnp.where(row < 2, ends, q), ROWS - 2, 0)
                        w1 = pltpu.roll(jnp.where(row >= ROWS - 1, ends, q), 1, 0)
                        w2 = pltpu.roll(jnp.where(row >= ROWS - 2, ends, q), 2, 0)
                        dy = moved[index, f, kk, :, lanes(t)]
                        sides = moved[index, f, kk, :, lanes(tiles + t)]
                        if t == 0:
                            dy = dy + jnp.where(lane < 2, extra_slope, 0.0)
                            sides = sides + jnp.where(lane < 1, extra_sum, 0.0)
                        if t == tiles - 1:
                            dy = dy + jnp.where(lane >= LANES - 2, extra_slope, 0.0)
                            sides = sides + jnp.where(lane >= LANES - 1, extra_sum, 0.0)
                        dx = 8.0 * (e1 - w1) - (e2 - w2)
                        per_tile.append((q, dx, dy, (e1 + w1) + sides))
                    fields.append(per_tile)
                for t in range(tiles):
                    live = active[t] > c * CHUNK + kk
                    (u, ux, uy, ul), (v, vx, vy, vl), (s, sx, sy, sl) = [
                        fields[f][t] for f in range(3)
                    ]
                    press_e[t] = press_e[t] + sx
                    press_n[t] = press_n[t] + sy
                    um = u * drift
                    vm = v * drift
                    news = [
                        (um * ux + vm * uy) + push * press_e[t] + (gain * CORIOLIS) * v
                        + (gain * VISCOSITY) * ul + keep_flow * u,
                        (um * vx + vm * vy) + push * press_n[t] - (gain * CORIOLIS) * u
                        + (gain * VISCOSITY) * vl + keep_flow * v,
                        (um * sx + vm * sy) + (gain * DIFFUSIVITY) * sl + keep_salt * s,
                    ]
                    for f in range(3):
                        new = news[f]
                        if weight0 is not None:
                            new = new + weight0 * held[c, f, kk, :, lanes(t)]
                        new = jnp.where(live, new, 0.0)
                        if stage < 2:
                            held[index + chunks, f, kk, :, lanes(t)] = new
                        else:
                            state_out[c, f, kk, :, lanes(t)] = new
                            if f < 2:
                                sums[f][t] = sums[f][t] + new
            if stage < 2:
                pack(stage + 1, c)
                launch(stage + 1, c)
            return (tuple(press_e), tuple(press_n)) + tuple(tuple(x) for x in sums)

        start = ((zero,) * tiles,) * (4 if stage == 2 else 2)
        if stage < 2:
            return lax.fori_loop(0, chunks, body, start)
        return lax.fori_loop(1, chunks, body, body(0, start, True))

    run_stage(0, None, 1.0)
    run_stage(1, 0.75, 0.25)
    far_start(0)
    carry = run_stage(2, 1.0 / 3.0, 2.0 / 3.0)

    put_far(1, [
        [floats[1, :, lanes(t)] * (carry[2 + f][t] / levels) for t in range(tiles)]
        for f in range(2)
    ])
    far_start(1)
    whole(gath.at[0], far_recv.at[0]).wait()

    wide = tiles + 1

    def window(kind, f):
        out = []
        for p in range(slots):
            line = [gath[kind, p, f * tiles + t] for t in range(tiles)]
            below = gath[kind, p, 2 * tiles]
            above = gath[kind, p, 2 * tiles + 1]
            if f == 1:
                above = pltpu.roll(above, LANES - RIM, 1)
                below = pltpu.roll(below, RIM, 1)
            line.append(
                jnp.where(lane < RIM, above, jnp.where(lane >= LANES - RIM, below, 0.0))
            )
            out.append(line)
        return out

    def up(z, p, t):
        after = z[p + 1][t] if p + 1 < slots else zero
        return pltpu.roll(jnp.where(row < 1, after, z[p][t]), ROWS - 1, 0)

    def down(z, p, t):
        before = z[p - 1][t] if p > 0 else zero
        return pltpu.roll(jnp.where(row >= ROWS - 1, before, z[p][t]), 1, 0)

    def right(z, p, t):
        return pltpu.roll(jnp.where(lane < 1, z[p][(t + 1) % wide], z[p][t]), LANES - 1, 1)

    def left(z, p, t):
        return pltpu.roll(jnp.where(lane >= LANES - 1, z[p][(t - 1) % wide], z[p][t]), 1, 1)

    def grid(make):
        return [[make(p, t) for t in range(wide)] for p in range(slots)]

    def box(w):
        b = grid(lambda p, t: 4.0 * w[p][t] + (up(w, p, t) + down(w, p, t)))
        return grid(lambda p, t: 4.0 * b[p][t] + (right(b, p, t) + left(b, p, t)))

    x = window(0, 0)
    wet = window(0, 1)
    wet6 = grid(lambda p, t: wet[p][t] * (1.0 / 6.0))
    w = grid(lambda p, t: wet[p][t] * x[p][t])
    image = box(w)
    start = grid(lambda p, t: wet6[p][t] * image[p][t] - 6.0 * w[p][t])

    whole(gath.at[1], far_recv.at[1]).wait()
    fe = window(1, 0)
    fn = window(1, 1)

    def right_side(p, t):
        div = (up(fe, p, t) - down(fe, p, t)) + (right(fn, p, t) - left(fn, p, t))
        return start[p][t] - wet[p][t] * ((0.5 * DIVERGENCE_COEF) * div)

    r = grid(right_side)
    d = grid(lambda p, t: r[p][t] * (1.0 / CHEB_CENTER))
    keeps, gains = cheb_table(ITERS)
    for index in range(ITERS):
        x = grid(lambda p, t: x[p][t] + d[p][t])
        if index < ITERS - 1:
            image = box(d)
            r = grid(
                lambda p, t: (r[p][t] - (SIGMA_SHIFT + 6.0) * d[p][t])
                + wet6[p][t] * image[p][t]
            )
            d = grid(lambda p, t: keeps[index] * d[p][t] + gains[index] * r[p][t])
    dry = dry_factor(ITERS)
    x = grid(lambda p, t: x[p][t] * (dry + (1.0 - dry) * wet[p][t]))

    for t in range(wide):
        xs[0, t] = zero
        xs[slots + 1, t] = zero
    for p in range(slots):
        for t in range(wide):
            xs[p + 1, t] = x[p][t]
    mine = [[xs[own + i, t] for t in range(wide)] for i in range(3)]
    for t in range(tiles):
        surface_out[:, lanes(t)] = mine[1][t]
        above = pltpu.roll(jnp.where(row < 1, mine[2][t], mine[1][t]), ROWS - 1, 0)
        below = pltpu.roll(jnp.where(row >= ROWS - 1, mine[0][t], mine[1][t]), 1, 0)
        slope_out[0, :, lanes(t)] = (above - below) * 0.5
        slope_out[1, :, lanes(t)] = (right(mine, 1, t) - left(mine, 1, t)) * 0.5

    for copy, side, there in near:
        @pl.when(there)
        def _(copy=copy, side=side):
            if copy is x_copy:
                whole(send_x.at[side], side_sem.at[side]).wait()
            else:
                whole(send_y, side_sem.at[2 + side]).wait()
    far(far_drain)


def finish(
    state_ref, slope_ref, surface_ref, wet_ref, active_ref,
    east_out, north_out, salt_out, surface_out, held, sems,
):
    early = (
        pltpu.make_async_copy(surface_ref, surface_out, sems.at[1]),
    ) + tuple(
        pltpu.make_async_copy(
            state_ref.at[c, 2], salt_out.at[pl.ds(c * CHUNK, CHUNK)], sems.at[4 + c]
        )
        for c in range(state_ref.shape[0])
    )
    for copy in early:
        copy.start()
    levels = held.shape[1]
    active = active_ref[...] * wet_ref[...]
    slopes = (slope_ref[0], slope_ref[1])
    for f in range(2):
        for k in range(levels):
            held[f, k] = jnp.where(
                active > k, state_ref[k // CHUNK, f, k % CHUNK] - slopes[f], 0.0
            )
        pltpu.make_async_copy(held.at[f], (east_out, north_out)[f], sems.at[2 + f]).start()
    for f in range(2):
        pltpu.make_async_copy(held.at[f], (east_out, north_out)[f], sems.at[2 + f]).wait()
    for copy in early:
        copy.wait()


def solution(mesh):
    nx, ny = mesh.shape["gx"], mesh.shape["gy"]

    def local(east, north, salt, surface, depth, wet, active):
        levels, rows, width = east.shape
        assert rows == ROWS and width % LANES == 0 and levels % CHUNK == 0
        assert ITERS + 2 <= RIM
        tiles = width // LANES
        chunks = levels // CHUNK
        n = 3 * CHUNK // 4 * tiles
        reach = min(nx - 1, -(-(ITERS + 2) // ROWS))
        slots = min(nx, 2 * reach + 1)
        f32 = jnp.float32
        vmem = pltpu.VMEM
        dma = pltpu.SemaphoreType.DMA
        block = pl.BlockSpec(memory_space=pltpu.VMEM)
        state = jax.ShapeDtypeStruct(east.shape, f32)
        hbm = pl.BlockSpec(memory_space=pltpu.HBM)
        tile = (rows, LANES)
        state3, slopes, surface_next = pl.pallas_call(
            functools.partial(kernel, nx, ny, reach, slots),
            out_shape=(
                jax.ShapeDtypeStruct((chunks, 3, CHUNK, rows, width), f32),
                jax.ShapeDtypeStruct((2,) + surface.shape, f32),
                jax.ShapeDtypeStruct(surface.shape, f32),
            ),
            in_specs=[hbm] * 7,
            out_specs=(block,) * 3,
            scratch_shapes=[
                vmem((3 * chunks, 3, CHUNK, rows, width), f32),
                vmem((3 * chunks, 3, CHUNK, rows, 2 * width), f32),
                vmem((width, 2 * width), jnp.bfloat16),
                vmem((2,) + surface.shape, jnp.int32),
                vmem((2,) + surface.shape, f32),
                vmem((n,) + tile, f32),
                vmem((3, chunks, 2 * n + 2) + tile, f32),
                vmem((2, 3, chunks, n) + tile, f32),
                vmem((3, chunks, 1) + tile, f32),
                vmem((2, 2 * tiles) + tile, f32),
                vmem((2, 1) + tile, f32),
                vmem((2, slots, 2 * tiles + 2) + tile, f32),
                vmem((slots + 2, tiles + 1) + tile, f32),
                dma((chunks,)),
                dma((2,)),
                dma((3, chunks)),
                dma((4,)),
                dma((3, slots)),
                dma((2,)),
            ],
            compiler_params=pltpu.CompilerParams(
                collective_id=0, has_side_effects=True, vmem_limit_bytes=48 * 1024 * 1024
            ),
        )(*[
            pltpu.with_memory_space_constraint(z, pltpu.HBM)
            for z in (east, north, salt, surface, depth, wet, active)
        ])
        return pl.pallas_call(
            finish,
            out_shape=(state, state, state, jax.ShapeDtypeStruct(surface.shape, f32)),
            in_specs=[block] * 5,
            out_specs=(hbm,) * 4,
            scratch_shapes=[vmem((2,) + east.shape, f32), dma((4 + chunks,))],
            compiler_params=pltpu.CompilerParams(vmem_limit_bytes=8 * 1024 * 1024),
        )(state3, slopes, surface_next, wet, active)

    return jax.shard_map(
        local,
        mesh=mesh,
        in_specs=(
            P(None, "gx", "gy"),
            P(None, "gx", "gy"),
            P(None, "gx", "gy"),
            P("gx", "gy"),
            P("gx", "gy"),
            P("gx", "gy"),
            P("gx", "gy"),
        ),
        out_specs=(P(None, "gx", "gy"), P(None, "gx", "gy"), P(None, "gx", "gy"), P("gx", "gy")),
        check_vma=False,
    )
```

profile of v0, /device:TPU:0, one launch (start us, length us, event | category | flops | bytes accessed | tf_op | source)
XLA Modules:
  0.0 24.3 jit_solution(3422263030540974446)
XLA Ops:
  0.6 0.0 copy-start.1
  0.6 0.0 copy-start
  0.7 22.5 %shard_map.102 = (f32[6,3,8,8,256]{4,3,2,1,0:T(8,128)S(1)}, f32[2,8,256]{2,1,0:T(8,128)S(1)}, f32[8,256]{1,0:T(8,128)S(1)}) custom-call(f32[48,8,256]{2,1,0:T(8,128)} %east_hbm.1, f32[48,8,256]{2,1,0:T(8,128)} %north_hbm.1, f32[48,8,256]{2,1,0:T(8,128)} %salt_hbm.1, f32[8,256]{1,0:T(8,128)} %surface_hbm.1, f32[8,256]{1,0:T(8,128)} %depth_hbm.1, ...), custom_call_target="tpu_custom_call" | custom-call | tf_op jit(solution)/shard_map/pallas_call | solution.py:562
  23.1 0.0 copy-done.1
  23.1 0.0 copy-done
  23.1 1.1 %shard_map.103 = (f32[48,8,256]{2,1,0:T(8,128)}, f32[48,8,256]{2,1,0:T(8,128)}, f32[48,8,256]{2,1,0:T(8,128)}, f32[8,256]{1,0:T(8,128)}) custom-call(f32[6,3,8,8,256]{4,3,2,1,0:T(8,128)S(1)} %get-tuple-element.7.state_ref, f32[2,8,256]{2,1,0:T(8,128)S(1)} %get-tuple-element.8.slope_ref, f32[8,256]{1,0:T(8,128)S(1)} %get-tuple-element.9.surface_ref, ...), custom_call_target="tpu_custom_call" | custom-call | tf_op jit(solution)/shard_map/pallas_call | solution.py:599
Async XLA Ops:
  0.6 22.5 %copy-start.1 = (s32[8,256]{1,0:T(8,128)S(1)}, s32[8,256]{1,0:T(8,128)}, u32[]{:S(2)}) copy-start(s32[8,256]{1,0:T(8,128)} %active_ref.1) | copy-start | bytes 24580
  0.6 22.5 %copy-start = (s32[8,256]{1,0:T(8,128)S(1)}, s32[8,256]{1,0:T(8,128)}, u32[]{:S(2)}) copy-start(s32[8,256]{1,0:T(8,128)} %wet_ref.1) | copy-start | bytes 24580
where the time goes:
time: 24.4 us; the launch traced here: 24.3 us
  Pallas kernels  23.6 us (97%)
  between operations  0.67 us (3%)
    pallas_call x1, Pallas kernels, local(): pl.pallas_call(functools.partial(kernel, nx, ny, reach, slots), out_shape...  22.5 us
    pallas_call x1, Pallas kernels, local(): pl.pallas_call(finish, out_shape=(state, state, state, jax.ShapeDtypeStru...  1.11 us

commit v1 on v0

--- a/solution.py
+++ b/solution.py
@@ -54,8 +54,8 @@
     nx, ny, reach, slots,
     east_hbm, north_hbm, salt_hbm, surface_hbm, depth_hbm, wet_hbm, active_hbm,
     state_out, slope_out, surface_out,
-    held, moved, shifts, ints, floats, zeros, halo, send_x, send_y, far_c, far_e, gath, xs,
-    load_sem, small_sem, halo_sem, side_sem, far_send, far_recv,
+    held, moved, shifts, ints, floats, halo, send_x, send_y, far_c, far_e, gath, xs,
+    block_count, rim_count, arrivals, blank, small_sem, halo_sem, side_sem, far_send, far_recv,
 ):
     gx = lax.axis_index("gx")
     gy = lax.axis_index("gy")
@@ -82,14 +82,14 @@
     def whole(ref, sem):
         return pltpu.make_async_copy(ref, ref, sem)
 
+    def load(c):
+        part = pl.ds(c * CHUNK, CHUNK)
+        for f, source in enumerate((east_hbm, north_hbm, salt_hbm)):
+            pltpu.make_async_copy(source.at[part], held.at[c, f], halo_sem.at[1, c]).start()
+
     pltpu.make_async_copy(active_hbm, ints.at[0], small_sem.at[0]).start()
     pltpu.make_async_copy(wet_hbm, ints.at[1], small_sem.at[0]).start()
-    for c in range(chunks):
-        part = pl.ds(c * CHUNK, CHUNK)
-        for f, source in enumerate((east_hbm, north_hbm, salt_hbm)):
-            pltpu.make_async_copy(source.at[part], held.at[c, f], load_sem.at[c]).start()
-    pltpu.make_async_copy(surface_hbm, floats.at[0], small_sem.at[1]).start()
-    pltpu.make_async_copy(depth_hbm, floats.at[1], small_sem.at[1]).start()
+    load(0)
 
     own = reach if relative else gx
     partners = [
@@ -98,6 +98,7 @@
         for side in (-1, 0, 1)
         if (o, side) != (0, 0)
     ]
+    partners.sort(key=lambda p: (-abs(p[1]), -abs(p[0])))
 
     def far(action):
         for o, side in partners:
@@ -105,6 +106,26 @@
             def _(o=o, side=side):
                 action(o, side)
 
+    def counts(size):
+        return (0,) if size == 1 else (1,) if size == 2 else (1, 2)
+
+    has_x = (gx > 0).astype(jnp.int32) + (gx < nx - 1).astype(jnp.int32)
+    has_y = (gy > 0).astype(jnp.int32) + (gy < ny - 1).astype(jnp.int32)
+
+    def arrive(stage, c):
+        for a in counts(nx):
+            for b in counts(ny):
+                @pl.when(jnp.logical_and(has_x == a, has_y == b))
+                def _(a=a, b=b):
+                    part = halo.at[stage, c, pl.ds(0, a * n + b)]
+                    whole(part, halo_sem.at[stage, c]).wait()
+
+    def far_arrive(kind):
+        for b in counts(ny):
+            @pl.when(has_y == b)
+            def _(b=b):
+                whole(arrivals.at[pl.ds(0, slots * (2 * tiles + b))], far_recv.at[kind]).wait()
+
     barrier = pltpu.get_barrier_semaphore()
     count = jnp.int32(0)
     for o, side in partners:
@@ -118,17 +139,10 @@
 
         count = count + there.astype(jnp.int32)
 
-    for i in range(n):
-        zeros[i] = zero
-
-    source = lax.broadcasted_iota(jnp.int32, (width, width), 0)
-    target = lax.broadcasted_iota(jnp.int32, (width, width), 1)
-    step = source - target
-    one = jnp.abs(step) == 1
-    sign = jnp.where(step > 0, 1.0, -1.0)
-    slope = jnp.where(one, 8.0 * sign, jnp.where(jnp.abs(step) == 2, -sign, 0.0))
-    shifts[:, :width] = slope.astype(jnp.bfloat16)
-    shifts[:, width:] = jnp.where(one, 1.0, 0.0).astype(jnp.bfloat16)
+    for c in range(1, chunks):
+        load(c)
+    pltpu.make_async_copy(surface_hbm, floats.at[0], small_sem.at[1]).start()
+    pltpu.make_async_copy(depth_hbm, floats.at[1], small_sem.at[1]).start()
 
     def move(index):
         value = held[index].reshape(3 * CHUNK * ROWS, width)
@@ -214,7 +228,7 @@
                 source, target = far_e.at[kind], gath.at[kind, slot, pl.ds(at, 1)]
             pltpu.make_async_remote_copy(
                 src_ref=source, dst_ref=target,
-                send_sem=far_send.at[side + 1, o + reach if relative else gx + o],
+                send_sem=far_send.at[side + 1, o + reach if relative else 0],
                 recv_sem=far_recv.at[kind],
                 device_id=(gx + o, gy + side), device_id_type=MESH,
             ).start()
@@ -225,8 +239,7 @@
         ).start()
 
     def far_drain(o, side):
-        sem = far_send.at[side + 1, o + reach if relative else gx + o]
-        whole(far_c if side == 0 else far_e, sem).wait()
+        whole(far_c if side == 0 else far_e, far_send.at[side + 1, o + reach]).wait()
 
     def fill_far(data):
         low, high = data
@@ -242,11 +255,30 @@
                 far_c[kind, f * tiles + t] = data[f][t]
         far_e[kind, 0] = fill_far(data)
 
+    for side, missing in ((0, gx == 0), (1, gx == nx - 1)):
+        @pl.when(missing)
+        def _(side=side):
+            for stage in range(3):
+                @pl.loop(0, chunks)
+                def _(c, stage=stage):
+                    halo[stage, c, side * n:(side + 1) * n] = jnp.zeros(
+                        (n, ROWS, LANES), jnp.float32
+                    )
+
+    for side, missing in ((0, gy == 0), (1, gy == ny - 1)):
+        @pl.when(missing)
+        def _(side=side):
+            halo[:, :, 2 * n + side] = jnp.zeros((3, chunks, ROWS, LANES), jnp.float32)
+            gath[:, :, 2 * tiles + side] = jnp.zeros((2, slots, ROWS, LANES), jnp.float32)
+
+    if relative:
+        blank[...] = jnp.zeros((2 * tiles, ROWS, LANES), jnp.float32)
+
     whole(ints, small_sem.at[0]).wait()
     active = [ints[0, :, lanes(t)] * ints[1, :, lanes(t)] for t in range(tiles)]
 
     def first(c):
-        whole(held.at[c], load_sem.at[c]).wait()
+        whole(held.at[c], halo_sem.at[1, c]).wait()
         for kk in range(CHUNK):
             for t in range(tiles):
                 live = active[t] > c * CHUNK + kk
@@ -264,38 +296,15 @@
     def _(c):
         first(c)
         launch(0, c)
-        move(c - 1)
-
-    for side, missing in ((0, gx == 0), (1, gx == nx - 1)):
-        @pl.when(missing)
-        def _(side=side):
-            for stage in range(3):
-                @pl.loop(0, chunks)
-                def _(c, stage=stage):
-                    pltpu.make_async_copy(
-                        zeros, halo.at[stage, c, pl.ds(side * n, n)], halo_sem.at[stage, c]
-                    ).start()
-
-    for side, missing in ((0, gy == 0), (1, gy == ny - 1)):
-        @pl.when(missing)
-        def _(side=side):
-            for stage in range(3):
-                @pl.loop(0, chunks)
-                def _(c, stage=stage):
-                    pltpu.make_async_copy(
-                        zeros.at[pl.ds(0, 1)],
-                        halo.at[stage, c, pl.ds(2 * n + side, 1)],
-                        halo_sem.at[stage, c],
-                    ).start()
-            for j in range(slots):
-                @pl.when(inside(gx + j - reach, gy) if relative else gy >= 0)
-                def _(j=j):
-                    for kind in range(2):
-                        pltpu.make_async_copy(
-                            zeros.at[pl.ds(0, 1)],
-                            gath.at[kind, j, pl.ds(2 * tiles + side, 1)],
-                            far_recv.at[kind],
-                        ).start()
+
+    source = lax.broadcasted_iota(jnp.int32, (width, width), 0)
+    target = lax.broadcasted_iota(jnp.int32, (width, width), 1)
+    step = source - target
+    one = jnp.abs(step) == 1
+    sign = jnp.where(step > 0, 1.0, -1.0)
+    slope = jnp.where(one, 8.0 * sign, jnp.where(jnp.abs(step) == 2, -sign, 0.0))
+    shifts[:, :width] = slope.astype(jnp.bfloat16)
+    shifts[:, width:] = jnp.where(one, 1.0, 0.0).astype(jnp.bfloat16)
 
     if relative:
         for j in range(slots):
@@ -303,14 +312,26 @@
             def _(j=j):
                 for kind in range(2):
                     pltpu.make_async_copy(
-                        zeros.at[pl.ds(0, 2 * tiles + 2)], gath.at[kind, j], far_recv.at[kind]
+                        blank, gath.at[kind, j, pl.ds(0, 2 * tiles)], far_recv.at[kind]
                     ).start()
+                    for side, there in ((0, gy > 0), (1, gy < ny - 1)):
+                        @pl.when(there)
+                        def _(kind=kind, side=side):
+                            pltpu.make_async_copy(
+                                blank.at[pl.ds(0, 1)],
+                                gath.at[kind, j, pl.ds(2 * tiles + side, 1)],
+                                far_recv.at[kind],
+                            ).start()
 
     whole(floats, small_sem.at[1]).wait()
     put_far(0, (
         [floats[0, :, lanes(t)] for t in range(tiles)],
         [ints[1, :, lanes(t)].astype(jnp.float32) for t in range(tiles)],
     ))
+
+    @pl.loop(0, chunks - 1)
+    def _(c):
+        move(c)
 
     quarter = lane % 4
 
@@ -325,7 +346,7 @@
             press_e, press_n = list(carry[0]), list(carry[1])
             sums = [list(x) for x in carry[2:]]
             index = stage * chunks + c
-            whole(halo.at[stage, c], halo_sem.at[stage, c]).wait()
+            arrive(stage, c)
             if behind:
                 move(index + chunks - 1)
             rims = jnp.where(quarter < 2, halo[stage, c, 2 * n], halo[stage, c, 2 * n + 1])
@@ -405,11 +426,12 @@
         start = ((zero,) * tiles,) * (4 if stage == 2 else 2)
         if stage < 2:
             return lax.fori_loop(0, chunks, body, start)
-        return lax.fori_loop(1, chunks, body, body(0, start, True))
+        start = body(0, start, True)
+        far_start(0)
+        return lax.fori_loop(1, chunks, body, start)
 
     run_stage(0, None, 1.0)
     run_stage(1, 0.75, 0.25)
-    far_start(0)
     carry = run_stage(2, 1.0 / 3.0, 2.0 / 3.0)
 
     put_far(1, [
@@ -417,7 +439,7 @@
         for f in range(2)
     ])
     far_start(1)
-    whole(gath.at[0], far_recv.at[0]).wait()
+    far_arrive(0)
 
     wide = tiles + 1
 
@@ -464,7 +486,7 @@
     image = box(w)
     start = grid(lambda p, t: wet6[p][t] * image[p][t] - 6.0 * w[p][t])
 
-    whole(gath.at[1], far_recv.at[1]).wait()
+    far_arrive(1)
     fe = window(1, 0)
     fn = window(1, 1)
 
@@ -508,7 +530,15 @@
                 whole(send_x.at[side], side_sem.at[side]).wait()
             else:
                 whole(send_y, side_sem.at[2 + side]).wait()
-    far(far_drain)
+    if relative:
+        far(far_drain)
+    else:
+        if nx > 1:
+            whole(block_count, far_send.at[1, 0]).wait()
+        for side, there in ((-1, gy > 0), (1, gy < ny - 1)):
+            @pl.when(there)
+            def _(side=side):
+                whole(rim_count, far_send.at[side + 1, 0]).wait()
 
 
 def finish(
@@ -574,7 +604,6 @@
                 vmem((width, 2 * width), jnp.bfloat16),
                 vmem((2,) + surface.shape, jnp.int32),
                 vmem((2,) + surface.shape, f32),
-                vmem((n,) + tile, f32),
                 vmem((3, chunks, 2 * n + 2) + tile, f32),
                 vmem((2, 3, chunks, n) + tile, f32),
                 vmem((3, chunks, 1) + tile, f32),
@@ -582,11 +611,14 @@
                 vmem((2, 1) + tile, f32),
                 vmem((2, slots, 2 * tiles + 2) + tile, f32),
                 vmem((slots + 2, tiles + 1) + tile, f32),
-                dma((chunks,)),
+                vmem((max(slots - 1, 1), 2, 2 * tiles) + tile, f32),
+                vmem((slots, 2, 1) + tile, f32),
+                vmem((slots * (2 * tiles + 2),) + tile, f32),
+                vmem((2 * tiles,) + tile, f32),
                 dma((2,)),
                 dma((3, chunks)),
                 dma((4,)),
-                dma((3, slots)),
+                dma((3, slots if slots < nx else 1)),
                 dma((2,)),
             ],
             compiler_params=pltpu.CompilerParams(

time: 24.4 us -> 24.1 us (0.988)
  Pallas kernels: 23.6 us -> 23.3 us
    pallas_call x1, Pallas kernels: 22.5 us -> 22.2 us  [local(): pl.pallas_call(functools.partial(kernel, nx, ny, reach, slots), out_shape...]
where the time goes in v1:
time: 24.1 us; the launch traced here: 23.9 us
  Pallas kernels  23.3 us (97%)
  between operations  0.67 us (3%)
    pallas_call x1, Pallas kernels, local(): pl.pallas_call(functools.partial(kernel, nx, ny, reach, slots), out_shape...  22.2 us
    pallas_call x1, Pallas kernels, local(): pl.pallas_call(finish, out_shape=(state, state, state, jax.ShapeDtypeStru...  1.11 us

profile of v1, /device:TPU:0, one launch (start us, length us, event | category | flops | bytes accessed | tf_op | source)
XLA Modules:
  0.0 23.9 jit_solution(10941139700656179914)
XLA Ops:
  0.6 0.0 copy-start.1
  0.6 0.0 copy-start
  0.7 22.2 %shard_map.102 = (f32[6,3,8,8,256]{4,3,2,1,0:T(8,128)S(1)}, f32[2,8,256]{2,1,0:T(8,128)S(1)}, f32[8,256]{1,0:T(8,128)S(1)}) custom-call(f32[48,8,256]{2,1,0:T(8,128)} %east_hbm.1, f32[48,8,256]{2,1,0:T(8,128)} %north_hbm.1, f32[48,8,256]{2,1,0:T(8,128)} %salt_hbm.1, f32[8,256]{1,0:T(8,128)} %surface_hbm.1, f32[8,256]{1,0:T(8,128)} %depth_hbm.1, ...), custom_call_target="tpu_custom_call" | custom-call | tf_op jit(solution)/shard_map/pallas_call | solution.py:592
  22.8 0.0 copy-done.1
  22.8 0.0 copy-done
  22.8 1.1 %shard_map.103 = (f32[48,8,256]{2,1,0:T(8,128)}, f32[48,8,256]{2,1,0:T(8,128)}, f32[48,8,256]{2,1,0:T(8,128)}, f32[8,256]{1,0:T(8,128)}) custom-call(f32[6,3,8,8,256]{4,3,2,1,0:T(8,128)S(1)} %get-tuple-element.7.state_ref, f32[2,8,256]{2,1,0:T(8,128)S(1)} %get-tuple-element.8.slope_ref, f32[8,256]{1,0:T(8,128)S(1)} %get-tuple-element.9.surface_ref, ...), custom_call_target="tpu_custom_call" | custom-call | tf_op jit(solution)/shard_map/pallas_call | solution.py:631
Async XLA Ops:
  0.6 22.2 %copy-start.1 = (s32[8,256]{1,0:T(8,128)S(1)}, s32[8,256]{1,0:T(8,128)}, u32[]{:S(2)}) copy-start(s32[8,256]{1,0:T(8,128)} %active_ref.1) | copy-start | bytes 24580
  0.6 22.2 %copy-start = (s32[8,256]{1,0:T(8,128)S(1)}, s32[8,256]{1,0:T(8,128)}, u32[]{:S(2)}) copy-start(s32[8,256]{1,0:T(8,128)} %wet_ref.1) | copy-start | bytes 24580

commit v2 on v1

--- a/solution.py
+++ b/solution.py
@@ -54,8 +54,9 @@
     nx, ny, reach, slots,
     east_hbm, north_hbm, salt_hbm, surface_hbm, depth_hbm, wet_hbm, active_hbm,
     state_out, slope_out, surface_out,
-    held, moved, shifts, ints, floats, halo, send_x, send_y, far_c, far_e, gath, xs,
+    held, moved, shifts, ints, floats, halo, send_x, send_y, far_c, far_e, stat_e, gath, xs,
     block_count, rim_count, arrivals, blank, small_sem, halo_sem, side_sem, far_send, far_recv,
+    rim_sem, relay_send, relay_recv,
 ):
     gx = lax.axis_index("gx")
     gy = lax.axis_index("gy")
@@ -120,11 +121,11 @@
                     part = halo.at[stage, c, pl.ds(0, a * n + b)]
                     whole(part, halo_sem.at[stage, c]).wait()
 
-    def far_arrive(kind):
+    def far_arrive():
         for b in counts(ny):
             @pl.when(has_y == b)
             def _(b=b):
-                whole(arrivals.at[pl.ds(0, slots * (2 * tiles + b))], far_recv.at[kind]).wait()
+                whole(arrivals.at[pl.ds(0, slots * (2 * tiles + b))], far_recv.at[0]).wait()
 
     barrier = pltpu.get_barrier_semaphore()
     count = jnp.int32(0)
@@ -150,41 +151,48 @@
         rest = value - high.astype(jnp.float32)
         middle = rest.astype(jnp.bfloat16)
         low = (rest - middle.astype(jnp.float32)).astype(jnp.bfloat16)
-        total = jnp.dot(low, shifts[...], preferred_element_type=jnp.float32)
-        total = total + jnp.dot(middle, shifts[...], preferred_element_type=jnp.float32)
-        total = total + jnp.dot(high, shifts[...], preferred_element_type=jnp.float32)
+        total = jnp.dot(
+            jnp.concatenate([low, middle, high], axis=1),
+            shifts[...],
+            preferred_element_type=jnp.float32,
+        )
         moved[index] = total.reshape(3, CHUNK, ROWS, 2 * width)
 
-    def pack(stage, c):
+    def pack(stage, c, half):
+        for f in range(3):
+            ups = [None] * tiles
+            downs = [None] * tiles
+            for m in range(4):
+                for t in range(tiles):
+                    part = held[stage * chunks + c, f, half * 4 + m, :, lanes(t)]
+                    turned = part if m == 3 else pltpu.roll(part, 2 * m + 2, 0)
+                    if m == 0:
+                        ups[t] = turned
+                        downs[t] = turned
+                    else:
+                        ups[t] = jnp.where(pair == m, turned, ups[t])
+                        downs[t] = jnp.where(pair == (m + 1) % 4, turned, downs[t])
+            for t in range(tiles):
+                at = (half * 3 + f) * tiles + t
+                send_x[0, stage, c, at] = downs[t]
+                send_x[1, stage, c, at] = ups[t]
+
+    def pack_rim(stage, c):
         rim = zero
         for f in range(3):
-            for half in range(CHUNK // 4):
-                group = f * (CHUNK // 4) + half
-                ups = [None] * tiles
-                downs = [None] * tiles
-                for m in range(4):
-                    kk = half * 4 + m
-                    position = group * 4 + m
-                    parts = [
-                        held[stage * chunks + c, f, kk, :, lanes(t)] for t in range(tiles)
-                    ]
-                    for t in range(tiles):
-                        turned = parts[t] if m == 3 else pltpu.roll(parts[t], 2 * m + 2, 0)
-                        if m == 0:
-                            ups[t] = turned
-                            downs[t] = turned
-                        else:
-                            ups[t] = jnp.where(pair == m, turned, ups[t])
-                            downs[t] = jnp.where(pair == (m + 1) % 4, turned, downs[t])
-                    ends = jnp.where(lane < LANES // 2, parts[0], parts[-1])
-                    rim = jnp.where(
-                        lane // 4 == position,
-                        pltpu.roll(ends, (4 * position + 2) % LANES, 1),
-                        rim,
-                    )
-                for t in range(tiles):
-                    send_x[0, stage, c, group * tiles + t] = downs[t]
-                    send_x[1, stage, c, group * tiles + t] = ups[t]
+            for kk in range(CHUNK):
+                position = f * CHUNK + kk
+                first, last = (
+                    held[stage * chunks + c, f, kk, :, lanes(t)] for t in (0, tiles - 1)
+                )
+                rim = jnp.where(
+                    lane // 4 == position,
+                    pltpu.roll(
+                        jnp.where(lane < LANES // 2, first, last),
+                        (4 * position + 2) % LANES, 1,
+                    ),
+                    rim,
+                )
         send_y[stage, c, 0] = rim
 
     def x_copy(stage, c, side):
@@ -207,39 +215,103 @@
             device_id_type=MESH,
         )
 
-    near = [
-        (x_copy, 0, gx > 0), (x_copy, 1, gx < nx - 1),
-        (y_copy, 0, gy > 0), (y_copy, 1, gy < ny - 1),
-    ]
-
-    def launch(stage, c):
-        for copy, side, there in near:
+    x_sides = ((0, gx > 0), (1, gx < nx - 1))
+    y_sides = ((0, gy > 0), (1, gy < ny - 1))
+
+    def launch_x(stage, c):
+        for half in range(CHUNK // 4):
+            pack(stage, c, half)
+        for side, there in x_sides:
             @pl.when(there)
-            def _(copy=copy, side=side):
-                copy(stage, c, side).start()
-
-    def far_start(kind):
+            def _(side=side):
+                x_copy(stage, c, side).start()
+
+    def launch_y(stage, c):
+        pack_rim(stage, c)
+        for side, there in y_sides:
+            @pl.when(there)
+            def _(side=side):
+                y_copy(stage, c, side).start()
+
+    def far_start():
         def action(o, side):
             slot = reach - o if relative else gx
             if side == 0:
-                source, target = far_c.at[kind], gath.at[kind, slot, pl.ds(0, 2 * tiles)]
+                source, target = far_c, gath.at[1, slot, pl.ds(0, 2 * tiles)]
             else:
                 at = 2 * tiles + (1 - side) // 2
-                source, target = far_e.at[kind], gath.at[kind, slot, pl.ds(at, 1)]
+                source, target = far_e, gath.at[1, slot, pl.ds(at, 1)]
             pltpu.make_async_remote_copy(
                 src_ref=source, dst_ref=target,
                 send_sem=far_send.at[side + 1, o + reach if relative else 0],
-                recv_sem=far_recv.at[kind],
+                recv_sem=far_recv.at[0],
                 device_id=(gx + o, gy + side), device_id_type=MESH,
             ).start()
 
         far(action)
         pltpu.make_async_copy(
-            far_c.at[kind], gath.at[kind, own, pl.ds(0, 2 * tiles)], far_recv.at[kind]
+            far_c, gath.at[1, own, pl.ds(0, 2 * tiles)], far_recv.at[0]
         ).start()
 
     def far_drain(o, side):
         whole(far_c if side == 0 else far_e, far_send.at[side + 1, o + reach]).wait()
+
+    def rim_start():
+        for side, there in y_sides:
+            @pl.when(there)
+            def _(side=side):
+                pltpu.make_async_remote_copy(
+                    src_ref=stat_e,
+                    dst_ref=gath.at[0, own, pl.ds(2 * tiles + 1 - side, 1)],
+                    send_sem=rim_sem.at[side], recv_sem=rim_sem.at[2],
+                    device_id=(gx, gy + 2 * side - 1), device_id_type=MESH,
+                ).start()
+
+    def rim_arrive():
+        for b in counts(ny):
+            @pl.when(has_y == b)
+            def _(b=b):
+                whole(arrivals.at[pl.ds(0, b)], rim_sem.at[2]).wait()
+        for side, there in y_sides:
+            @pl.when(there)
+            def _(side=side):
+                whole(stat_e, rim_sem.at[side]).wait()
+
+    def relay_steps(action, step):
+        for side, there in x_sides:
+            sign = 2 * side - 1
+            passed = gx - sign * (step - 1)
+            sends = jnp.logical_and(there, jnp.logical_and(passed >= 0, passed < nx))
+            comes = jnp.logical_and(gx - sign * step >= 0, gx - sign * step < nx)
+            action(side, sign, sends, comes)
+
+    def relay(step):
+        def action(side, sign, sends, comes):
+            @pl.when(sends)
+            def _():
+                source = own - sign * (step - 1)
+                target = own - sign * step if relative else source
+                pltpu.make_async_remote_copy(
+                    src_ref=gath.at[0, source], dst_ref=gath.at[0, target],
+                    send_sem=relay_send.at[side], recv_sem=relay_recv.at[side, step - 1],
+                    device_id=(gx + sign, gy), device_id_type=MESH,
+                ).start()
+
+        relay_steps(action, step)
+
+    def relay_arrive(step):
+        def action(side, sign, sends, comes):
+            @pl.when(comes)
+            def _():
+                whole(
+                    gath.at[0, own - sign * step], relay_recv.at[side, step - 1]
+                ).wait()
+
+            @pl.when(sends)
+            def _():
+                whole(gath.at[0, own - sign * (step - 1)], relay_send.at[side]).wait()
+
+        relay_steps(action, step)
 
     def fill_far(data):
         low, high = data
@@ -249,11 +321,10 @@
         )
         return jnp.where(lane < 2 * RIM, first, second)
 
-    def put_far(kind, data):
+    def put(target, data):
         for f in range(2):
             for t in range(tiles):
-                far_c[kind, f * tiles + t] = data[f][t]
-        far_e[kind, 0] = fill_far(data)
+                target[f * tiles + t] = data[f][t]
 
     for side, missing in ((0, gx == 0), (1, gx == nx - 1)):
         @pl.when(missing)
@@ -286,16 +357,19 @@
                     held[c, f, kk, :, lanes(t)] = jnp.where(
                         live, held[c, f, kk, :, lanes(t)], 0.0
                     )
-        pack(0, c)
+
+    def first_launch(c):
+        launch_y(0, c)
+        launch_x(0, c)
 
     first(0)
     pl.semaphore_wait(barrier, count)
-    launch(0, 0)
+    first_launch(0)
 
     @pl.loop(1, chunks)
     def _(c):
         first(c)
-        launch(0, c)
+        first_launch(c)
 
     source = lax.broadcasted_iota(jnp.int32, (width, width), 0)
     target = lax.broadcasted_iota(jnp.int32, (width, width), 1)
@@ -303,31 +377,36 @@
     one = jnp.abs(step) == 1
     sign = jnp.where(step > 0, 1.0, -1.0)
     slope = jnp.where(one, 8.0 * sign, jnp.where(jnp.abs(step) == 2, -sign, 0.0))
-    shifts[:, :width] = slope.astype(jnp.bfloat16)
-    shifts[:, width:] = jnp.where(one, 1.0, 0.0).astype(jnp.bfloat16)
+    for i in range(3):
+        part = slice(i * width, (i + 1) * width)
+        shifts[part, :width] = slope.astype(jnp.bfloat16)
+        shifts[part, width:] = jnp.where(one, 1.0, 0.0).astype(jnp.bfloat16)
 
     if relative:
         for j in range(slots):
             @pl.when(jnp.logical_not(inside(gx + j - reach, gy)))
             def _(j=j):
-                for kind in range(2):
-                    pltpu.make_async_copy(
-                        blank, gath.at[kind, j, pl.ds(0, 2 * tiles)], far_recv.at[kind]
-                    ).start()
-                    for side, there in ((0, gy > 0), (1, gy < ny - 1)):
-                        @pl.when(there)
-                        def _(kind=kind, side=side):
-                            pltpu.make_async_copy(
-                                blank.at[pl.ds(0, 1)],
-                                gath.at[kind, j, pl.ds(2 * tiles + side, 1)],
-                                far_recv.at[kind],
-                            ).start()
+                gath[0, j] = jnp.zeros((2 * tiles + 2, ROWS, LANES), jnp.float32)
+                pltpu.make_async_copy(
+                    blank, gath.at[1, j, pl.ds(0, 2 * tiles)], far_recv.at[0]
+                ).start()
+                for side, there in y_sides:
+                    @pl.when(there)
+                    def _(side=side):
+                        pltpu.make_async_copy(
+                            blank.at[pl.ds(0, 1)],
+                            gath.at[1, j, pl.ds(2 * tiles + side, 1)],
+                            far_recv.at[0],
+                        ).start()
 
     whole(floats, small_sem.at[1]).wait()
-    put_far(0, (
+    stats = (
         [floats[0, :, lanes(t)] for t in range(tiles)],
         [ints[1, :, lanes(t)].astype(jnp.float32) for t in range(tiles)],
-    ))
+    )
+    put(gath.at[0, own], stats)
+    stat_e[0] = fill_far(stats)
+    rim_start()
 
     @pl.loop(0, chunks - 1)
     def _(c):
@@ -362,7 +441,7 @@
                 fields = []
                 for f in range(3):
                     position = f * CHUNK + kk
-                    group, m = position // 4, position % 4
+                    group, m = (kk // 4) * 3 + f, kk % 4
                     back = (-(4 * position + 2)) % LANES
                     extra_slope = pltpu.roll(rim_slope, back, 1)
                     extra_sum = pltpu.roll(rim_sum, back, 1)
@@ -419,27 +498,38 @@
                             if f < 2:
                                 sums[f][t] = sums[f][t] + new
             if stage < 2:
-                pack(stage + 1, c)
-                launch(stage + 1, c)
+                launch_y(stage + 1, c)
+                launch_x(stage + 1, c)
             return (tuple(press_e), tuple(press_n)) + tuple(tuple(x) for x in sums)
 
         start = ((zero,) * tiles,) * (4 if stage == 2 else 2)
         if stage < 2:
             return lax.fori_loop(0, chunks, body, start)
-        start = body(0, start, True)
-        far_start(0)
-        return lax.fori_loop(1, chunks, body, start)
+        return lax.fori_loop(1, chunks, body, body(0, start, True))
+
+    def pass_on(step):
+        if step == 1:
+            rim_arrive()
+        elif step - 1 <= reach:
+            relay_arrive(step - 1)
+        if step <= reach:
+            relay(step)
 
     run_stage(0, None, 1.0)
+    pass_on(1)
     run_stage(1, 0.75, 0.25)
+    pass_on(2)
     carry = run_stage(2, 1.0 / 3.0, 2.0 / 3.0)
 
-    put_far(1, [
+    flows = [
         [floats[1, :, lanes(t)] * (carry[2 + f][t] / levels) for t in range(tiles)]
         for f in range(2)
-    ])
-    far_start(1)
-    far_arrive(0)
+    ]
+    put(far_c, flows)
+    far_e[0] = fill_far(flows)
+    far_start()
+    pass_on(3)
+    pass_on(4)
 
     wide = tiles + 1
 
@@ -486,7 +576,7 @@
     image = box(w)
     start = grid(lambda p, t: wet6[p][t] * image[p][t] - 6.0 * w[p][t])
 
-    far_arrive(1)
+    far_arrive()
     fe = window(1, 0)
     fn = window(1, 1)
 
@@ -523,13 +613,16 @@
         slope_out[0, :, lanes(t)] = (above - below) * 0.5
         slope_out[1, :, lanes(t)] = (right(mine, 1, t) - left(mine, 1, t)) * 0.5
 
-    for copy, side, there in near:
+    for side, there in x_sides:
         @pl.when(there)
-        def _(copy=copy, side=side):
-            if copy is x_copy:
-                whole(send_x.at[side], side_sem.at[side]).wait()
-            else:
-                whole(send_y, side_sem.at[2 + side]).wait()
+        def _(side=side):
+            whole(send_x.at[side], side_sem.at[side]).wait()
+
+    for side, there in y_sides:
+        @pl.when(there)
+        def _(side=side):
+            whole(send_y, side_sem.at[2 + side]).wait()
+
     if relative:
         far(far_drain)
     else:
@@ -576,7 +669,7 @@
     def local(east, north, salt, surface, depth, wet, active):
         levels, rows, width = east.shape
         assert rows == ROWS and width % LANES == 0 and levels % CHUNK == 0
-        assert ITERS + 2 <= RIM
+        assert ITERS + 2 <= RIM and ITERS + 2 <= 3 * ROWS
         tiles = width // LANES
         chunks = levels // CHUNK
         n = 3 * CHUNK // 4 * tiles
@@ -601,25 +694,29 @@
             scratch_shapes=[
                 vmem((3 * chunks, 3, CHUNK, rows, width), f32),
                 vmem((3 * chunks, 3, CHUNK, rows, 2 * width), f32),
-                vmem((width, 2 * width), jnp.bfloat16),
+                vmem((3 * width, 2 * width), jnp.bfloat16),
                 vmem((2,) + surface.shape, jnp.int32),
                 vmem((2,) + surface.shape, f32),
                 vmem((3, chunks, 2 * n + 2) + tile, f32),
                 vmem((2, 3, chunks, n) + tile, f32),
                 vmem((3, chunks, 1) + tile, f32),
-                vmem((2, 2 * tiles) + tile, f32),
-                vmem((2, 1) + tile, f32),
+                vmem((2 * tiles,) + tile, f32),
+                vmem((1,) + tile, f32),
+                vmem((1,) + tile, f32),
                 vmem((2, slots, 2 * tiles + 2) + tile, f32),
                 vmem((slots + 2, tiles + 1) + tile, f32),
-                vmem((max(slots - 1, 1), 2, 2 * tiles) + tile, f32),
-                vmem((slots, 2, 1) + tile, f32),
+                vmem((max(slots - 1, 1), 2 * tiles) + tile, f32),
+                vmem((slots,) + tile, f32),
                 vmem((slots * (2 * tiles + 2),) + tile, f32),
                 vmem((2 * tiles,) + tile, f32),
                 dma((2,)),
                 dma((3, chunks)),
                 dma((4,)),
                 dma((3, slots if slots < nx else 1)),
+                dma((1,)),
+                dma((3,)),
                 dma((2,)),
+                dma((2, max(reach, 1))),
             ],
             compiler_params=pltpu.CompilerParams(
                 collective_id=0, has_side_effects=True, vmem_limit_bytes=48 * 1024 * 1024

time: 24.1 us -> 24.3 us (level)
  no operation moved by 1% of the time
where the time goes in v2:
time: 24.3 us; the launch traced here: 24.1 us
  Pallas kernels  23.4 us (96%)
  between operations  0.67 us (3%)
    pallas_call x1, Pallas kernels, local(): pl.pallas_call(functools.partial(kernel, nx, ny, reach, slots), out_shape...  22.3 us
    pallas_call x1, Pallas kernels, local(): pl.pallas_call(finish, out_shape=(state, state, state, jax.ShapeDtypeStru...  1.11 us

profile of v2, /device:TPU:0, one launch (start us, length us, event | category | flops | bytes accessed | tf_op | source)
XLA Modules:
  0.0 24.1 jit_solution(6336175769551356142)
XLA Ops:
  0.6 0.0 copy-start.1
  0.6 0.0 copy-start
  0.7 22.3 %shard_map.102 = (f32[6,3,8,8,256]{4,3,2,1,0:T(8,128)S(1)}, f32[2,8,256]{2,1,0:T(8,128)S(1)}, f32[8,256]{1,0:T(8,128)S(1)}) custom-call(f32[48,8,256]{2,1,0:T(8,128)} %east_hbm.1, f32[48,8,256]{2,1,0:T(8,128)} %north_hbm.1, f32[48,8,256]{2,1,0:T(8,128)} %salt_hbm.1, f32[8,256]{1,0:T(8,128)} %surface_hbm.1, f32[8,256]{1,0:T(8,128)} %depth_hbm.1, ...), custom_call_target="tpu_custom_call" | custom-call | tf_op jit(solution)/shard_map/pallas_call | solution.py:685
  23.0 0.0 copy-done.1
  23.0 0.0 copy-done
  23.0 1.1 %shard_map.103 = (f32[48,8,256]{2,1,0:T(8,128)}, f32[48,8,256]{2,1,0:T(8,128)}, f32[48,8,256]{2,1,0:T(8,128)}, f32[8,256]{1,0:T(8,128)}) custom-call(f32[6,3,8,8,256]{4,3,2,1,0:T(8,128)S(1)} %get-tuple-element.7.state_ref, f32[2,8,256]{2,1,0:T(8,128)S(1)} %get-tuple-element.8.slope_ref, f32[8,256]{1,0:T(8,128)S(1)} %get-tuple-element.9.surface_ref, ...), custom_call_target="tpu_custom_call" | custom-call | tf_op jit(solution)/shard_map/pallas_call | solution.py:728
Async XLA Ops:
  0.6 22.3 %copy-start.1 = (s32[8,256]{1,0:T(8,128)S(1)}, s32[8,256]{1,0:T(8,128)}, u32[]{:S(2)}) copy-start(s32[8,256]{1,0:T(8,128)} %active_ref.1) | copy-start | bytes 24580
  0.6 22.3 %copy-start = (s32[8,256]{1,0:T(8,128)S(1)}, s32[8,256]{1,0:T(8,128)}, u32[]{:S(2)}) copy-start(s32[8,256]{1,0:T(8,128)} %wet_ref.1) | copy-start | bytes 24580

commit v3 on v2

--- a/solution.py
+++ b/solution.py
@@ -129,7 +129,7 @@
 
     barrier = pltpu.get_barrier_semaphore()
     count = jnp.int32(0)
-    for o, side in partners:
+    for o, side in ((-1, 0), (1, 0), (0, -1), (0, 1)):
         there = inside(gx + o, gy + side)
 
         @pl.when(there)

time: 24.3 us -> 24.2 us (level)
  no operation moved by 1% of the time
where the time goes in v3:
time: 24.2 us; the launch traced here: 24 us
  Pallas kernels  23.3 us (96%)
  between operations  0.67 us (3%)
    pallas_call x1, Pallas kernels, local(): pl.pallas_call(functools.partial(kernel, nx, ny, reach, slots), out_shape...  22.2 us
    pallas_call x1, Pallas kernels, local(): pl.pallas_call(finish, out_shape=(state, state, state, jax.ShapeDtypeStru...  1.11 us

profile of v3, /device:TPU:0, one launch (start us, length us, event | category | flops | bytes accessed | tf_op | source)
XLA Modules:
  0.0 24.0 jit_solution(201326695493289416)
XLA Ops:
  0.6 0.0 copy-start.1
  0.6 0.0 copy-start
  0.7 22.2 %shard_map.102 = (f32[6,3,8,8,256]{4,3,2,1,0:T(8,128)S(1)}, f32[2,8,256]{2,1,0:T(8,128)S(1)}, f32[8,256]{1,0:T(8,128)S(1)}) custom-call(f32[48,8,256]{2,1,0:T(8,128)} %east_hbm.1, f32[48,8,256]{2,1,0:T(8,128)} %north_hbm.1, f32[48,8,256]{2,1,0:T(8,128)} %salt_hbm.1, f32[8,256]{1,0:T(8,128)} %surface_hbm.1, f32[8,256]{1,0:T(8,128)} %depth_hbm.1, ...), custom_call_target="tpu_custom_call" | custom-call | tf_op jit(solution)/shard_map/pallas_call | solution.py:685
  22.9 0.0 copy-done.1
  22.9 0.0 copy-done
  22.9 1.1 %shard_map.103 = (f32[48,8,256]{2,1,0:T(8,128)}, f32[48,8,256]{2,1,0:T(8,128)}, f32[48,8,256]{2,1,0:T(8,128)}, f32[8,256]{1,0:T(8,128)}) custom-call(f32[6,3,8,8,256]{4,3,2,1,0:T(8,128)S(1)} %get-tuple-element.7.state_ref, f32[2,8,256]{2,1,0:T(8,128)S(1)} %get-tuple-element.8.slope_ref, f32[8,256]{1,0:T(8,128)S(1)} %get-tuple-element.9.surface_ref, ...), custom_call_target="tpu_custom_call" | custom-call | tf_op jit(solution)/shard_map/pallas_call | solution.py:728
Async XLA Ops:
  0.6 22.3 %copy-start.1 = (s32[8,256]{1,0:T(8,128)S(1)}, s32[8,256]{1,0:T(8,128)}, u32[]{:S(2)}) copy-start(s32[8,256]{1,0:T(8,128)} %active_ref.1) | copy-start | bytes 24580
  0.6 22.3 %copy-start = (s32[8,256]{1,0:T(8,128)S(1)}, s32[8,256]{1,0:T(8,128)}, u32[]{:S(2)}) copy-start(s32[8,256]{1,0:T(8,128)} %wet_ref.1) | copy-start | bytes 24580

commit v4 on v3

--- a/solution.py
+++ b/solution.py
@@ -88,10 +88,6 @@
         for f, source in enumerate((east_hbm, north_hbm, salt_hbm)):
             pltpu.make_async_copy(source.at[part], held.at[c, f], halo_sem.at[1, c]).start()
 
-    pltpu.make_async_copy(active_hbm, ints.at[0], small_sem.at[0]).start()
-    pltpu.make_async_copy(wet_hbm, ints.at[1], small_sem.at[0]).start()
-    load(0)
-
     own = reach if relative else gx
     partners = [
         (o, side)
@@ -119,7 +115,7 @@
                 @pl.when(jnp.logical_and(has_x == a, has_y == b))
                 def _(a=a, b=b):
                     part = halo.at[stage, c, pl.ds(0, a * n + b)]
-                    whole(part, halo_sem.at[stage, c]).wait()
+                    whole(part, halo_sem.at[stage % 2, c]).wait()
 
     def far_arrive():
         for b in counts(ny):
@@ -140,10 +136,20 @@
 
         count = count + there.astype(jnp.int32)
 
-    for c in range(1, chunks):
-        load(c)
-    pltpu.make_async_copy(surface_hbm, floats.at[0], small_sem.at[1]).start()
-    pltpu.make_async_copy(depth_hbm, floats.at[1], small_sem.at[1]).start()
+    pltpu.make_async_copy(active_hbm, ints.at[0], small_sem.at[0]).start()
+    pltpu.make_async_copy(wet_hbm, ints.at[1], small_sem.at[0]).start()
+    load(0)
+
+    source = lax.broadcasted_iota(jnp.int32, (width, width), 0)
+    target = lax.broadcasted_iota(jnp.int32, (width, width), 1)
+    step = source - target
+    one = jnp.abs(step) == 1
+    sign = jnp.where(step > 0, 1.0, -1.0)
+    slope = jnp.where(one, 8.0 * sign, jnp.where(jnp.abs(step) == 2, -sign, 0.0))
+    for i in range(3):
+        part = slice(i * width, (i + 1) * width)
+        shifts[part, :width] = slope.astype(jnp.bfloat16)
+        shifts[part, width:] = jnp.where(one, 1.0, 0.0).astype(jnp.bfloat16)
 
     def move(index):
         value = held[index].reshape(3 * CHUNK * ROWS, width)
@@ -200,7 +206,7 @@
             src_ref=send_x.at[side, stage, c],
             dst_ref=halo.at[stage, c, pl.ds((1 - side) * n, n)],
             send_sem=side_sem.at[side],
-            recv_sem=halo_sem.at[stage, c],
+            recv_sem=halo_sem.at[stage % 2, c],
             device_id=(gx + 2 * side - 1, gy),
             device_id_type=MESH,
         )
@@ -210,7 +216,7 @@
             src_ref=send_y.at[stage, c],
             dst_ref=halo.at[stage, c, pl.ds(2 * n + 1 - side, 1)],
             send_sem=side_sem.at[2 + side],
-            recv_sem=halo_sem.at[stage, c],
+            recv_sem=halo_sem.at[stage % 2, c],
             device_id=(gx, gy + 2 * side - 1),
             device_id_type=MESH,
         )
@@ -218,20 +224,18 @@
     x_sides = ((0, gx > 0), (1, gx < nx - 1))
     y_sides = ((0, gy > 0), (1, gy < ny - 1))
 
-    def launch_x(stage, c):
+    def launch(stage, c):
         for half in range(CHUNK // 4):
             pack(stage, c, half)
-        for side, there in x_sides:
-            @pl.when(there)
-            def _(side=side):
-                x_copy(stage, c, side).start()
-
-    def launch_y(stage, c):
         pack_rim(stage, c)
         for side, there in y_sides:
             @pl.when(there)
             def _(side=side):
                 y_copy(stage, c, side).start()
+        for side, there in x_sides:
+            @pl.when(there)
+            def _(side=side):
+                x_copy(stage, c, side).start()
 
     def far_start():
         def action(o, side):
@@ -358,29 +362,18 @@
                         live, held[c, f, kk, :, lanes(t)], 0.0
                     )
 
-    def first_launch(c):
-        launch_y(0, c)
-        launch_x(0, c)
-
     first(0)
+    for c in range(1, chunks):
+        load(c)
+    pltpu.make_async_copy(surface_hbm, floats.at[0], small_sem.at[1]).start()
+    pltpu.make_async_copy(depth_hbm, floats.at[1], small_sem.at[1]).start()
     pl.semaphore_wait(barrier, count)
-    first_launch(0)
+    launch(0, 0)
 
     @pl.loop(1, chunks)
     def _(c):
         first(c)
-        first_launch(c)
-
-    source = lax.broadcasted_iota(jnp.int32, (width, width), 0)
-    target = lax.broadcasted_iota(jnp.int32, (width, width), 1)
-    step = source - target
-    one = jnp.abs(step) == 1
-    sign = jnp.where(step > 0, 1.0, -1.0)
-    slope = jnp.where(one, 8.0 * sign, jnp.where(jnp.abs(step) == 2, -sign, 0.0))
-    for i in range(3):
-        part = slice(i * width, (i + 1) * width)
-        shifts[part, :width] = slope.astype(jnp.bfloat16)
-        shifts[part, width:] = jnp.where(one, 1.0, 0.0).astype(jnp.bfloat16)
+        launch(0, c)
 
     if relative:
         for j in range(slots):
@@ -498,8 +491,7 @@
                             if f < 2:
                                 sums[f][t] = sums[f][t] + new
             if stage < 2:
-                launch_y(stage + 1, c)
-                launch_x(stage + 1, c)
+                launch(stage + 1, c)
             return (tuple(press_e), tuple(press_n)) + tuple(tuple(x) for x in sums)
 
         start = ((zero,) * tiles,) * (4 if stage == 2 else 2)
@@ -526,7 +518,7 @@
         for f in range(2)
     ]
     put(far_c, flows)
-    far_e[0] = fill_far(flows)
+    far_e[0] = fill_far(flows[::-1])
     far_start()
     pass_on(3)
     pass_on(4)
@@ -539,7 +531,7 @@
             line = [gath[kind, p, f * tiles + t] for t in range(tiles)]
             below = gath[kind, p, 2 * tiles]
             above = gath[kind, p, 2 * tiles + 1]
-            if f == 1:
+            if f != kind:
                 above = pltpu.roll(above, LANES - RIM, 1)
                 below = pltpu.roll(below, RIM, 1)
             line.append(
@@ -710,7 +702,7 @@
                 vmem((slots * (2 * tiles + 2),) + tile, f32),
                 vmem((2 * tiles,) + tile, f32),
                 dma((2,)),
-                dma((3, chunks)),
+                dma((2, chunks)),
                 dma((4,)),
                 dma((3, slots if slots < nx else 1)),
                 dma((1,)),

time: 24.2 us -> 24 us (level)
  no operation moved by 1% of the time
where the time goes in v4:
time: 24 us; the launch traced here: 23.8 us
  Pallas kernels  23.1 us (96%)
  between operations  0.67 us (3%)
    pallas_call x1, Pallas kernels, local(): pl.pallas_call(functools.partial(kernel, nx, ny, reach, slots), out_shape...  22 us
    pallas_call x1, Pallas kernels, local(): pl.pallas_call(finish, out_shape=(state, state, state, jax.ShapeDtypeStru...  1.11 us

profile of v4, /device:TPU:0, one launch (start us, length us, event | category | flops | bytes accessed | tf_op | source)
XLA Modules:
  0.0 23.8 jit_solution(10613360609665775208)
XLA Ops:
  0.6 0.0 copy-start.1
  0.6 0.0 copy-start
  0.7 22.0 %shard_map.102 = (f32[6,3,8,8,256]{4,3,2,1,0:T(8,128)S(1)}, f32[2,8,256]{2,1,0:T(8,128)S(1)}, f32[8,256]{1,0:T(8,128)S(1)}) custom-call(f32[48,8,256]{2,1,0:T(8,128)} %east_hbm.1, f32[48,8,256]{2,1,0:T(8,128)} %north_hbm.1, f32[48,8,256]{2,1,0:T(8,128)} %salt_hbm.1, f32[8,256]{1,0:T(8,128)} %surface_hbm.1, f32[8,256]{1,0:T(8,128)} %depth_hbm.1, ...), custom_call_target="tpu_custom_call" | custom-call | tf_op jit(solution)/shard_map/pallas_call | solution.py:677
  22.7 0.0 copy-done.1
  22.7 0.0 copy-done
  22.7 1.1 %shard_map.103 = (f32[48,8,256]{2,1,0:T(8,128)}, f32[48,8,256]{2,1,0:T(8,128)}, f32[48,8,256]{2,1,0:T(8,128)}, f32[8,256]{1,0:T(8,128)}) custom-call(f32[6,3,8,8,256]{4,3,2,1,0:T(8,128)S(1)} %get-tuple-element.7.state_ref, f32[2,8,256]{2,1,0:T(8,128)S(1)} %get-tuple-element.8.slope_ref, f32[8,256]{1,0:T(8,128)S(1)} %get-tuple-element.9.surface_ref, ...), custom_call_target="tpu_custom_call" | custom-call | tf_op jit(solution)/shard_map/pallas_call | solution.py:720
Async XLA Ops:
  0.6 22.1 %copy-start.1 = (s32[8,256]{1,0:T(8,128)S(1)}, s32[8,256]{1,0:T(8,128)}, u32[]{:S(2)}) copy-start(s32[8,256]{1,0:T(8,128)} %active_ref.1) | copy-start | bytes 24580
  0.6 22.1 %copy-start = (s32[8,256]{1,0:T(8,128)S(1)}, s32[8,256]{1,0:T(8,128)}, u32[]{:S(2)}) copy-start(s32[8,256]{1,0:T(8,128)} %wet_ref.1) | copy-start | bytes 24580

commit v5 on v4

--- a/solution.py
+++ b/solution.py
@@ -55,7 +55,7 @@
     east_hbm, north_hbm, salt_hbm, surface_hbm, depth_hbm, wet_hbm, active_hbm,
     state_out, slope_out, surface_out,
     held, moved, shifts, ints, floats, halo, send_x, send_y, far_c, far_e, stat_e, gath, xs,
-    block_count, rim_count, arrivals, blank, small_sem, halo_sem, side_sem, far_send, far_recv,
+    block_count, rim_count, y_count, arrivals, blank, halo_sem, side_sem, far_send, far_recv,
     rim_sem, relay_send, relay_recv,
 ):
     gx = lax.axis_index("gx")
@@ -95,7 +95,7 @@
         for side in (-1, 0, 1)
         if (o, side) != (0, 0)
     ]
-    partners.sort(key=lambda p: (-abs(p[1]), -abs(p[0])))
+    partners.sort(key=lambda p: (-abs(p[1]), p[0] != 0, -abs(p[0])))
 
     def far(action):
         for o, side in partners:
@@ -136,8 +136,8 @@
 
         count = count + there.astype(jnp.int32)
 
-    pltpu.make_async_copy(active_hbm, ints.at[0], small_sem.at[0]).start()
-    pltpu.make_async_copy(wet_hbm, ints.at[1], small_sem.at[0]).start()
+    pltpu.make_async_copy(active_hbm, ints.at[0], relay_recv.at[0, 0]).start()
+    pltpu.make_async_copy(wet_hbm, ints.at[1], relay_recv.at[0, 0]).start()
     load(0)
 
     source = lax.broadcasted_iota(jnp.int32, (width, width), 0)
@@ -199,13 +199,13 @@
                     ),
                     rim,
                 )
-        send_y[stage, c, 0] = rim
+        return rim
 
     def x_copy(stage, c, side):
         return pltpu.make_async_remote_copy(
             src_ref=send_x.at[side, stage, c],
             dst_ref=halo.at[stage, c, pl.ds((1 - side) * n, n)],
-            send_sem=side_sem.at[side],
+            send_sem=side_sem.at[0],
             recv_sem=halo_sem.at[stage % 2, c],
             device_id=(gx + 2 * side - 1, gy),
             device_id_type=MESH,
@@ -215,7 +215,7 @@
         return pltpu.make_async_remote_copy(
             src_ref=send_y.at[stage, c],
             dst_ref=halo.at[stage, c, pl.ds(2 * n + 1 - side, 1)],
-            send_sem=side_sem.at[2 + side],
+            send_sem=side_sem.at[1],
             recv_sem=halo_sem.at[stage % 2, c],
             device_id=(gx, gy + 2 * side - 1),
             device_id_type=MESH,
@@ -227,15 +227,16 @@
     def launch(stage, c):
         for half in range(CHUNK // 4):
             pack(stage, c, half)
-        pack_rim(stage, c)
+        rim = pack_rim(stage, c)
+        for side, there in x_sides:
+            @pl.when(there)
+            def _(side=side):
+                x_copy(stage, c, side).start()
+        send_y[stage, c, 0] = rim
         for side, there in y_sides:
             @pl.when(there)
             def _(side=side):
                 y_copy(stage, c, side).start()
-        for side, there in x_sides:
-            @pl.when(there)
-            def _(side=side):
-                x_copy(stage, c, side).start()
 
     def far_start():
         def action(o, side):
@@ -267,7 +268,7 @@
                 pltpu.make_async_remote_copy(
                     src_ref=stat_e,
                     dst_ref=gath.at[0, own, pl.ds(2 * tiles + 1 - side, 1)],
-                    send_sem=rim_sem.at[side], recv_sem=rim_sem.at[2],
+                    send_sem=relay_send.at[side], recv_sem=rim_sem.at[0],
                     device_id=(gx, gy + 2 * side - 1), device_id_type=MESH,
                 ).start()
 
@@ -275,11 +276,11 @@
         for b in counts(ny):
             @pl.when(has_y == b)
             def _(b=b):
-                whole(arrivals.at[pl.ds(0, b)], rim_sem.at[2]).wait()
+                whole(arrivals.at[pl.ds(0, b)], rim_sem.at[0]).wait()
         for side, there in y_sides:
             @pl.when(there)
             def _(side=side):
-                whole(stat_e, rim_sem.at[side]).wait()
+                whole(stat_e, relay_send.at[side]).wait()
 
     def relay_steps(action, step):
         for side, there in x_sides:
@@ -349,7 +350,7 @@
     if relative:
         blank[...] = jnp.zeros((2 * tiles, ROWS, LANES), jnp.float32)
 
-    whole(ints, small_sem.at[0]).wait()
+    whole(ints, relay_recv.at[0, 0]).wait()
     active = [ints[0, :, lanes(t)] * ints[1, :, lanes(t)] for t in range(tiles)]
 
     def first(c):
@@ -365,8 +366,8 @@
     first(0)
     for c in range(1, chunks):
         load(c)
-    pltpu.make_async_copy(surface_hbm, floats.at[0], small_sem.at[1]).start()
-    pltpu.make_async_copy(depth_hbm, floats.at[1], small_sem.at[1]).start()
+    pltpu.make_async_copy(surface_hbm, floats.at[0], relay_recv.at[0, 1]).start()
+    pltpu.make_async_copy(depth_hbm, floats.at[1], relay_recv.at[0, 1]).start()
     pl.semaphore_wait(barrier, count)
     launch(0, 0)
 
@@ -392,7 +393,7 @@
                             far_recv.at[0],
                         ).start()
 
-    whole(floats, small_sem.at[1]).wait()
+    whole(floats, relay_recv.at[0, 1]).wait()
     stats = (
         [floats[0, :, lanes(t)] for t in range(tiles)],
         [ints[1, :, lanes(t)].astype(jnp.float32) for t in range(tiles)],
@@ -605,15 +606,15 @@
         slope_out[0, :, lanes(t)] = (above - below) * 0.5
         slope_out[1, :, lanes(t)] = (right(mine, 1, t) - left(mine, 1, t)) * 0.5
 
-    for side, there in x_sides:
-        @pl.when(there)
-        def _(side=side):
-            whole(send_x.at[side], side_sem.at[side]).wait()
-
-    for side, there in y_sides:
-        @pl.when(there)
-        def _(side=side):
-            whole(send_y, side_sem.at[2 + side]).wait()
+    for a in counts(nx):
+        @pl.when(jnp.logical_and(has_x == a, has_x > 0))
+        def _(a=a):
+            whole(send_x.at[pl.ds(0, max(a, 1))], side_sem.at[0]).wait()
+
+    for b in counts(ny):
+        @pl.when(jnp.logical_and(has_y == b, has_y > 0))
+        def _(b=b):
+            whole(y_count.at[pl.ds(0, max(b, 1))], side_sem.at[1]).wait()
 
     if relative:
         far(far_drain)
@@ -699,16 +700,16 @@
                 vmem((slots + 2, tiles + 1) + tile, f32),
                 vmem((max(slots - 1, 1), 2 * tiles) + tile, f32),
                 vmem((slots,) + tile, f32),
+                vmem((2, 3, chunks, 1) + tile, f32),
                 vmem((slots * (2 * tiles + 2),) + tile, f32),
                 vmem((2 * tiles,) + tile, f32),
+                dma((2, chunks)),
                 dma((2,)),
-                dma((2, chunks)),
-                dma((4,)),
                 dma((3, slots if slots < nx else 1)),
                 dma((1,)),
-                dma((3,)),
+                dma((1,)),
                 dma((2,)),
-                dma((2, max(reach, 1))),
+                dma((2, max(reach, 2))),
             ],
             compiler_params=pltpu.CompilerParams(
                 collective_id=0, has_side_effects=True, vmem_limit_bytes=48 * 1024 * 1024

time: 24 us -> 23.9 us (level)
  no operation moved by 1% of the time
where the time goes in v5:
time: 23.9 us; the launch traced here: 23.7 us
  Pallas kernels  23 us (96%)
  between operations  0.67 us (3%)
    pallas_call x1, Pallas kernels, local(): pl.pallas_call(functools.partial(kernel, nx, ny, reach, slots), out_shape...  21.9 us
    pallas_call x1, Pallas kernels, local(): pl.pallas_call(finish, out_shape=(state, state, state, jax.ShapeDtypeStru...  1.11 us

profile of v5, /device:TPU:0, one launch (start us, length us, event | category | flops | bytes accessed | tf_op | source)
XLA Modules:
  0.0 23.7 jit_solution(6659792124771436986)
XLA Ops:
  0.6 0.0 copy-start.1
  0.6 0.0 copy-start
  0.7 21.9 %shard_map.102 = (f32[6,3,8,8,256]{4,3,2,1,0:T(8,128)S(1)}, f32[2,8,256]{2,1,0:T(8,128)S(1)}, f32[8,256]{1,0:T(8,128)S(1)}) custom-call(f32[48,8,256]{2,1,0:T(8,128)} %east_hbm.1, f32[48,8,256]{2,1,0:T(8,128)} %north_hbm.1, f32[48,8,256]{2,1,0:T(8,128)} %salt_hbm.1, f32[8,256]{1,0:T(8,128)} %surface_hbm.1, f32[8,256]{1,0:T(8,128)} %depth_hbm.1, ...), custom_call_target="tpu_custom_call" | custom-call | tf_op jit(solution)/shard_map/pallas_call | solution.py:678
  22.6 0.0 copy-done.1
  22.6 0.0 copy-done
  22.6 1.1 %shard_map.103 = (f32[48,8,256]{2,1,0:T(8,128)}, f32[48,8,256]{2,1,0:T(8,128)}, f32[48,8,256]{2,1,0:T(8,128)}, f32[8,256]{1,0:T(8,128)}) custom-call(f32[6,3,8,8,256]{4,3,2,1,0:T(8,128)S(1)} %get-tuple-element.7.state_ref, f32[2,8,256]{2,1,0:T(8,128)S(1)} %get-tuple-element.8.slope_ref, f32[8,256]{1,0:T(8,128)S(1)} %get-tuple-element.9.surface_ref, ...), custom_call_target="tpu_custom_call" | custom-call | tf_op jit(solution)/shard_map/pallas_call | solution.py:721
Async XLA Ops:
  0.6 22.0 %copy-start.1 = (s32[8,256]{1,0:T(8,128)S(1)}, s32[8,256]{1,0:T(8,128)}, u32[]{:S(2)}) copy-start(s32[8,256]{1,0:T(8,128)} %active_ref.1) | copy-start | bytes 24580
  0.6 22.0 %copy-start = (s32[8,256]{1,0:T(8,128)S(1)}, s32[8,256]{1,0:T(8,128)}, u32[]{:S(2)}) copy-start(s32[8,256]{1,0:T(8,128)} %wet_ref.1) | copy-start | bytes 24580

commit v6 on v5

--- a/solution.py
+++ b/solution.py
@@ -55,7 +55,7 @@
     east_hbm, north_hbm, salt_hbm, surface_hbm, depth_hbm, wet_hbm, active_hbm,
     state_out, slope_out, surface_out,
     held, moved, shifts, ints, floats, halo, send_x, send_y, far_c, far_e, stat_e, gath, xs,
-    block_count, rim_count, y_count, arrivals, blank, halo_sem, side_sem, far_send, far_recv,
+    y_count, arrivals, blank, halo_sem, side_sem, far_send, far_recv,
     rim_sem, relay_send, relay_recv,
 ):
     gx = lax.axis_index("gx")
@@ -248,7 +248,7 @@
                 source, target = far_e, gath.at[1, slot, pl.ds(at, 1)]
             pltpu.make_async_remote_copy(
                 src_ref=source, dst_ref=target,
-                send_sem=far_send.at[side + 1, o + reach if relative else 0],
+                send_sem=far_send.at[side + 1, o + reach] if relative else far_send.at[0, 0],
                 recv_sem=far_recv.at[0],
                 device_id=(gx + o, gy + side), device_id_type=MESH,
             ).start()
@@ -619,28 +619,23 @@
     if relative:
         far(far_drain)
     else:
-        if nx > 1:
-            whole(block_count, far_send.at[1, 0]).wait()
-        for side, there in ((-1, gy > 0), (1, gy < ny - 1)):
-            @pl.when(there)
-            def _(side=side):
-                whole(rim_count, far_send.at[side + 1, 0]).wait()
+        for b in counts(ny):
+            @pl.when(has_y == b)
+            def _(b=b):
+                sent = (slots - 1) * 2 * tiles + b * slots
+                whole(arrivals.at[pl.ds(0, sent)], far_send.at[0, 0]).wait()
 
 
 def finish(
     state_ref, slope_ref, surface_ref, wet_ref, active_ref,
     east_out, north_out, salt_out, surface_out, held, sems,
 ):
-    early = (
-        pltpu.make_async_copy(surface_ref, surface_out, sems.at[1]),
-    ) + tuple(
+    surface_copy = pltpu.make_async_copy(surface_ref, surface_out, sems.at[1])
+    surface_copy.start()
+    for c in range(state_ref.shape[0]):
         pltpu.make_async_copy(
-            state_ref.at[c, 2], salt_out.at[pl.ds(c * CHUNK, CHUNK)], sems.at[4 + c]
-        )
-        for c in range(state_ref.shape[0])
-    )
-    for copy in early:
-        copy.start()
+            state_ref.at[c, 2], salt_out.at[pl.ds(c * CHUNK, CHUNK)], sems.at[0]
+        ).start()
     levels = held.shape[1]
     active = active_ref[...] * wet_ref[...]
     slopes = (slope_ref[0], slope_ref[1])
@@ -649,11 +644,9 @@
             held[f, k] = jnp.where(
                 active > k, state_ref[k // CHUNK, f, k % CHUNK] - slopes[f], 0.0
             )
-        pltpu.make_async_copy(held.at[f], (east_out, north_out)[f], sems.at[2 + f]).start()
-    for f in range(2):
-        pltpu.make_async_copy(held.at[f], (east_out, north_out)[f], sems.at[2 + f]).wait()
-    for copy in early:
-        copy.wait()
+        pltpu.make_async_copy(held.at[f], (east_out, north_out)[f], sems.at[0]).start()
+    pltpu.make_async_copy(held, held, sems.at[0]).wait()
+    surface_copy.wait()
 
 
 def solution(mesh):
@@ -698,14 +691,12 @@
                 vmem((1,) + tile, f32),
                 vmem((2, slots, 2 * tiles + 2) + tile, f32),
                 vmem((slots + 2, tiles + 1) + tile, f32),
-                vmem((max(slots - 1, 1), 2 * tiles) + tile, f32),
-                vmem((slots,) + tile, f32),
                 vmem((2, 3, chunks, 1) + tile, f32),
                 vmem((slots * (2 * tiles + 2),) + tile, f32),
                 vmem((2 * tiles,) + tile, f32),
                 dma((2, chunks)),
                 dma((2,)),
-                dma((3, slots if slots < nx else 1)),
+                dma((3, slots) if slots < nx else (1, 1)),
                 dma((1,)),
                 dma((1,)),
                 dma((2,)),
@@ -723,7 +714,7 @@
             out_shape=(state, state, state, jax.ShapeDtypeStruct(surface.shape, f32)),
             in_specs=[block] * 5,
             out_specs=(hbm,) * 4,
-            scratch_shapes=[vmem((2,) + east.shape, f32), dma((4 + chunks,))],
+            scratch_shapes=[vmem((3,) + east.shape, f32), dma((2,))],
             compiler_params=pltpu.CompilerParams(vmem_limit_bytes=8 * 1024 * 1024),
         )(state3, slopes, surface_next, wet, active)
 

time: 23.9 us -> 23.8 us (level)
  no operation moved by 1% of the time
where the time goes in v6:
time: 23.8 us; the launch traced here: 23.6 us
  Pallas kernels  22.9 us (96%)
  between operations  0.67 us (3%)
    pallas_call x1, Pallas kernels, local(): pl.pallas_call(functools.partial(kernel, nx, ny, reach, slots), out_shape...  21.9 us
    pallas_call x1, Pallas kernels, local(): pl.pallas_call(finish, out_shape=(state, state, state, jax.ShapeDtypeStru...  1.03 us

profile of v6, /device:TPU:0, one launch (start us, length us, event | category | flops | bytes accessed | tf_op | source)
XLA Modules:
  0.0 23.6 jit_solution(10095282478629871243)
XLA Ops:
  0.6 0.0 copy-start.1
  0.6 0.0 copy-start
  0.7 21.9 %shard_map.102 = (f32[6,3,8,8,256]{4,3,2,1,0:T(8,128)S(1)}, f32[2,8,256]{2,1,0:T(8,128)S(1)}, f32[8,256]{1,0:T(8,128)S(1)}) custom-call(f32[48,8,256]{2,1,0:T(8,128)} %east_hbm.1, f32[48,8,256]{2,1,0:T(8,128)} %north_hbm.1, f32[48,8,256]{2,1,0:T(8,128)} %salt_hbm.1, f32[8,256]{1,0:T(8,128)} %surface_hbm.1, f32[8,256]{1,0:T(8,128)} %depth_hbm.1, ...), custom_call_target="tpu_custom_call" | custom-call | tf_op jit(solution)/shard_map/pallas_call | solution.py:671
  22.6 0.0 copy-done.1
  22.6 0.0 copy-done
  22.6 1.0 %shard_map.103 = (f32[48,8,256]{2,1,0:T(8,128)}, f32[48,8,256]{2,1,0:T(8,128)}, f32[48,8,256]{2,1,0:T(8,128)}, f32[8,256]{1,0:T(8,128)}) custom-call(f32[6,3,8,8,256]{4,3,2,1,0:T(8,128)S(1)} %get-tuple-element.7.state_ref, f32[2,8,256]{2,1,0:T(8,128)S(1)} %get-tuple-element.8.slope_ref, f32[8,256]{1,0:T(8,128)S(1)} %get-tuple-element.9.surface_ref, ...), custom_call_target="tpu_custom_call" | custom-call | tf_op jit(solution)/shard_map/pallas_call | solution.py:712
Async XLA Ops:
  0.6 21.9 %copy-start.1 = (s32[8,256]{1,0:T(8,128)S(1)}, s32[8,256]{1,0:T(8,128)}, u32[]{:S(2)}) copy-start(s32[8,256]{1,0:T(8,128)} %active_ref.1) | copy-start | bytes 24580
  0.6 21.9 %copy-start = (s32[8,256]{1,0:T(8,128)S(1)}, s32[8,256]{1,0:T(8,128)}, u32[]{:S(2)}) copy-start(s32[8,256]{1,0:T(8,128)} %wet_ref.1) | copy-start | bytes 24580
